TPU v7x, 32 devices: a whole 2x2x4 slice. The times are simulated.
32 devices in a mesh: gx: 2 (over y), gy: 4 (over x, core), gz: 4 (over z).
Axes of the slice: x: 2, y: 2, z: 4, core: 2. Of those that a mesh axis runs over, the one named last changes fastest.
Arguments:
- node_latents: bfloat16 [32768, 128], P(('gx', 'gy', 'gz')), may hold values from -300 to 300
- cluster_latents: bfloat16 [8192, 128], P(('gx', 'gy', 'gz')), may hold values from -6 to 6
- senders: int32 [1024, 128], P(('gx', 'gy', 'gz')), may hold values from 0 to 4095
- membership: int32 [32768], P(('gx', 'gy', 'gz')), may hold values from 0 to 255
- w_key: bfloat16 [128, 128], replicated, may hold values from -1 to 1
- w_value: bfloat16 [128, 128], replicated, may hold values from -0.5 to 0.5
- w_edge_in: bfloat16 [256, 128], replicated, may hold values from -0.375 to 0.375
- w_edge_out: bfloat16 [128, 128], replicated, may hold values from -0.5 to 0.5
- w_node_in: bfloat16 [512, 128], replicated, may hold values from -0.25 to 0.25
- w_node_out: bfloat16 [128, 128], replicated, may hold values from -0.5 to 0.5
- out_gain: float32 [128], replicated, may hold values from 0.5 to 1.5
Outputs:
- new_latents: bfloat16 [32768, 128], P(('gx', 'gy', 'gz'))
All inputs are finite; a program needn't handle non-finite values.
Results may differ from a plain program's by a relative error of at most 0.005.
Values may be sent and summed in bfloat16 or wider, within the bound.
A program may use at most 64 MiB of HBM per device.

v0:
```python
import jax
import jax.numpy as jnp
from jax import lax
from jax.sharding import PartitionSpec as P

BND = 512


NEG_FILL = -1e30


def extended_2(cells, sides, width):
    for axis, dim in sides:
        count = lax.axis_size(axis)
        head = lax.slice_in_dim(cells, 0, width, axis=dim)
        tail = lax.slice_in_dim(cells, cells.shape[dim] - width, cells.shape[dim], axis=dim)
        cells = jnp.concatenate(
            [
                lax.ppermute(tail, axis, [(i, (i + 1) % count) for i in range(count)]),
                cells,
                lax.ppermute(head, axis, [((i + 1) % count, i) for i in range(count)]),
            ],
            axis=dim,
        )
    return cells


def project(latent_rows, weight):
    return jnp.dot(latent_rows, weight, preferred_element_type=jnp.float32).astype(jnp.bfloat16)


def absorb_into(carry, key_rows, value_rows, queries):
    running_max, running_sum, weighted = carry
    scores = lax.dot_general(
        queries, key_rows, (((1,), (1,)), ((), ())), preferred_element_type=jnp.float32
    )
    scores = scores / jnp.sqrt(jnp.float32(queries.shape[1]))
    newest = jnp.maximum(running_max, jnp.max(scores, axis=1))
    exponent = jnp.exp(scores - newest[:, None])
    running_sum = jnp.sum(exponent, axis=1)
    weighted = jnp.dot(
        exponent.astype(jnp.bfloat16), value_rows, preferred_element_type=jnp.float32
    )
    return (newest, running_sum, weighted)


def on_device(
    node_latents,
    cluster_latents,
    senders,
    membership,
    w_key,
    w_value,
    w_edge_in,
    w_edge_out,
    w_node_in,
    w_node_out,
    out_gain,
):
    count, width = node_latents.shape
    start_carry = (
        jnp.full((count,), NEG_FILL, jnp.float32),
        jnp.zeros((count,), jnp.float32),
        jnp.zeros((count, width), jnp.float32),
    )
    key_rows = project(cluster_latents, w_key)
    value_rows = project(cluster_latents, w_value)

    def visit_pairs(carry, portion):
        return absorb_into(carry, portion[0], portion[1], node_latents)

    along_x = visit_pairs(
        start_carry,
        (
            lax.all_gather(key_rows, "gx", axis=0, tiled=True),
            lax.all_gather(value_rows, "gx", axis=0, tiled=True),
        ),
    )
    along_y = visit_pairs(
        start_carry,
        (
            lax.all_gather(key_rows, "gy", axis=0, tiled=True),
            lax.all_gather(value_rows, "gy", axis=0, tiled=True),
        ),
    )
    along_z = visit_pairs(
        start_carry,
        (
            lax.all_gather(key_rows, "gz", axis=0, tiled=True),
            lax.all_gather(value_rows, "gz", axis=0, tiled=True),
        ),
    )
    pooled = (
        along_x[2] / along_x[1][:, None]
        + along_y[2] / along_y[1][:, None]
        + along_z[2] / along_z[1][:, None]
    )
    attended = (
        pooled * lax.rsqrt(jnp.mean(pooled * pooled, axis=1, keepdims=True) + 1e-06)
    ).astype(jnp.bfloat16)
    border = node_latents[:BND].reshape(1, 1, 1, BND, width)
    padded = extended_2(border, (("gx", 0), ("gy", 1), ("gz", 2)), 1)
    extended = jnp.concatenate(
        [
            node_latents,
            padded[0, 1, 1],
            padded[2, 1, 1],
            padded[1, 0, 1],
            padded[1, 2, 1],
            padded[1, 1, 0],
            padded[1, 1, 2],
        ],
        axis=0,
    )
    sender_rows = jnp.take(extended, senders.reshape(-1), axis=0)
    degree = senders.size // count
    receiver_part = jnp.dot(node_latents, w_edge_in[:width], preferred_element_type=jnp.float32)
    sender_part = jnp.dot(sender_rows, w_edge_in[width:], preferred_element_type=jnp.float32)
    edge_hidden = jax.nn.silu(
        sender_part.reshape(count, degree, width) + receiver_part[:, None, :]
    ).astype(jnp.bfloat16)
    messages = jnp.dot(
        edge_hidden.reshape(count * degree, width), w_edge_out, preferred_element_type=jnp.float32
    )
    aggregated = jnp.sum(messages.reshape(count, degree, width), axis=1).astype(jnp.bfloat16)
    clusters_here = cluster_latents.shape[0]
    one_hot = (membership[:, None] == jnp.arange(clusters_here, dtype=jnp.int32)[None, :]).astype(
        jnp.bfloat16
    )
    own_cluster = jnp.dot(one_hot, cluster_latents, preferred_element_type=jnp.float32).astype(
        jnp.bfloat16
    )
    preact = jnp.dot(node_latents, w_node_in[:width], preferred_element_type=jnp.float32)
    preact = preact + jnp.dot(
        aggregated, w_node_in[width : 2 * width], preferred_element_type=jnp.float32
    )
    preact = preact + jnp.dot(
        attended, w_node_in[2 * width : 3 * width], preferred_element_type=jnp.float32
    )
    preact = preact + jnp.dot(
        own_cluster, w_node_in[3 * width :], preferred_element_type=jnp.float32
    )
    node_hidden = jax.nn.silu(preact).astype(jnp.bfloat16)
    update = jnp.dot(node_hidden, w_node_out, preferred_element_type=jnp.float32)
    centred = update - jnp.mean(update, axis=1, keepdims=True)
    variance = jnp.mean(centred * centred, axis=1, keepdims=True)
    normed = centred * lax.rsqrt(variance + 1e-05)
    return (node_latents.astype(jnp.float32) + normed * out_gain).astype(jnp.bfloat16)


def solution(mesh):
    in_specs = (
        P(("gx", "gy", "gz"), None),
        P(("gx", "gy", "gz"), None),
        P(("gx", "gy", "gz"), None),
        P(("gx", "gy", "gz")),
        P(),
        P(),
        P(),
        P(),
        P(),
        P(),
        P(),
    )
    out_specs = P(("gx", "gy", "gz"), None)
    return jax.shard_map(
        on_device, mesh=mesh, in_specs=in_specs, out_specs=out_specs, check_vma=False
    )
```

profile of v0, /device:TPU:0, one launch (start us, length us, event | category | flops | bytes accessed | tf_op | source)
XLA Modules:
  0.0 145.5 jit_solution(14745661145467966139)
XLA Ops:
  0.0 1.0 slice_bitcast_fusion.4
  1.0 3.1 %collective-permute-start = (bf16[1,1,1,512,128]{4,3,2,1,0:T(8,128)(2,1)S(1)}, bf16[1,1,1,512,128]{4,3,2,1,0:T(8,128)(2,1)S(1)}, u32[]{:S(2)}, u32[]{:S(2)}) collective-permute-start(bf16[1,1,1,512,128]{4,3,2,1,0:T(8,128)(2,1)S(1)} %slice_bitcast_fusion.4), channel_id=1, source_target_pairs={{0,16},{16,0},{1,17},{17,1},{2,18},{18,2},{3,19},{19,3},{4,20},{20... | collective-permute-start | bytes 393224 | tf_op jit(solution)/shard_map/ppermute | solution.py:19
  4.1 0.1 collective-permute-start.1
  4.1 0.9 convolution_convert_fusion.2
  5.0 6.2 %all_gather.20 = bf16[1024,128]{1,0:T(8,128)(2,1)S(1)} all-gather(bf16[256,128]{1,0:T(8,128)(2,1)S(1)} %convolution_convert_fusion.2), channel_id=1, replica_groups=mesh['gx'=2,'gy'=4,'gz'=4] {'gy'}, dimensions={0}, use_global_device_ids=true | all-gather | bytes 327680 | tf_op jit(solution)/shard_map/all_gather | solution.py:82
  11.2 14.1 %all_gather.22 = bf16[1024,128]{1,0:T(8,128)(2,1)S(1)} all-gather(bf16[256,128]{1,0:T(8,128)(2,1)S(1)} %convolution_convert_fusion.2), channel_id=1, replica_groups=mesh['gx'=2,'gy'=4,'gz'=4] {'gz'}, dimensions={0}, use_global_device_ids=true | all-gather | bytes 327680 | tf_op jit(solution)/shard_map/all_gather | solution.py:89
  25.3 0.9 convolution_convert_fusion.1
  26.2 5.8 %all_gather.21 = bf16[1024,128]{1,0:T(8,128)(2,1)S(1)} all-gather(bf16[256,128]{1,0:T(8,128)(2,1)S(1)} %convolution_convert_fusion.1), channel_id=1, replica_groups=mesh['gx'=2,'gy'=4,'gz'=4] {'gy'}, dimensions={0}, use_global_device_ids=true | all-gather | bytes 327680 | tf_op jit(solution)/shard_map/all_gather | solution.py:83
  32.0 14.4 %all_gather.23 = bf16[1024,128]{1,0:T(8,128)(2,1)S(1)} all-gather(bf16[256,128]{1,0:T(8,128)(2,1)S(1)} %convolution_convert_fusion.1), channel_id=1, replica_groups=mesh['gx'=2,'gy'=4,'gz'=4] {'gz'}, dimensions={0}, use_global_device_ids=true | all-gather | bytes 327680 | tf_op jit(solution)/shard_map/all_gather | solution.py:90
  46.4 4.9 %all_gather.18 = bf16[512,128]{1,0:T(8,128)(2,1)S(1)} all-gather(bf16[256,128]{1,0:T(8,128)(2,1)S(1)} %convolution_convert_fusion.2), channel_id=1, replica_groups=mesh['gx'=2,'gy'=4,'gz'=4] {'gx'}, dimensions={0}, use_global_device_ids=true | all-gather | bytes 196608 | tf_op jit(solution)/shard_map/all_gather | solution.py:75
  51.4 0.2 fusion.41
  51.6 1.0 fusion.44
  52.6 0.7 multiply_reduce_fusion.1
  53.3 0.7 multiply_reduce_fusion
  54.0 0.4 multiply_reduce_fusion.2
  54.5 0.7 fusion
  55.2 0.9 fusion.16
  56.1 0.7 fusion.2
  56.9 0.9 fusion.19
  57.8 0.1 collective-permute-start.2
  57.9 1.7 %collective-permute-start.3 = (bf16[3,1,1,512,128]{4,3,2,1,0:T(8,128)(2,1)S(1)}, bf16[3,1,1,512,128]{4,3,2,1,0:T(8,128)(2,1)S(1)}, u32[]{:S(2)}, u32[]{:S(2)}) collective-permute-start(bf16[3,1,1,512,128]{4,3,2,1,0:T(8,128)(2,1)S(1)} %pad_maximum_fusion.1), channel_id=1, source_target_pairs={{4,0},{8,4},{12,8},{0,12},{5,1},{9,5},{13,9},{1,13},{6,2},{10,6},{... | collective-permute-start | bytes 1179656 | tf_op jit(solution)/shard_map/ppermute | solution.py:21
  59.6 0.4 fusion.12
  60.0 4.9 %all_gather.19 = bf16[512,128]{1,0:T(8,128)(2,1)S(1)} all-gather(bf16[256,128]{1,0:T(8,128)(2,1)S(1)} %convolution_convert_fusion.1), channel_id=1, replica_groups=mesh['gx'=2,'gy'=4,'gz'=4] {'gx'}, dimensions={0}, use_global_device_ids=true | all-gather | bytes 196608 | tf_op jit(solution)/shard_map/all_gather | solution.py:76
  64.9 1.3 multiply_reduce_fusion.4
  66.2 1.3 collective-permute-done.2
  67.5 0.8 collective-permute-done.3
  68.3 1.1 pad_maximum_fusion
  69.4 2.2 %collective-permute-start.4 = (bf16[3,3,1,512,128]{4,3,2,1,0:T(8,128)(2,1)}, bf16[3,3,1,512,128]{4,3,2,1,0:T(8,128)(2,1)}, u32[]{:S(2)}, u32[]{:S(2)}) collective-permute-start(bf16[3,3,1,512,128]{4,3,2,1,0:T(8,128)(2,1)} %pad_maximum_fusion), channel_id=1, source_target_pairs={{0,1},{1,2},{2,3},{3,0},{4,5},{5,6},{6,7},{7,4},{8,9},{9,10},{10,1... | collective-permute-start | bytes 3538952 | tf_op jit(solution)/shard_map/ppermute | solution.py:19
  71.7 1.9 %collective-permute-start.5 = (bf16[3,3,1,512,128]{4,3,2,1,0:T(8,128)(2,1)}, bf16[3,3,1,512,128]{4,3,2,1,0:T(8,128)(2,1)}, u32[]{:S(2)}, u32[]{:S(2)}) collective-permute-start(bf16[3,3,1,512,128]{4,3,2,1,0:T(8,128)(2,1)} %pad_maximum_fusion), channel_id=1, source_target_pairs={{1,0},{2,1},{3,2},{0,3},{5,4},{6,5},{7,6},{4,7},{9,8},{10,9},{11,1... | collective-permute-start | bytes 3538952 | tf_op jit(solution)/shard_map/ppermute | solution.py:21
  73.6 0.9 copy.14
  74.5 26.1 %collective-permute-done.4 = bf16[3,3,1,512,128]{4,3,2,1,0:T(8,128)(2,1)} collective-permute-done((bf16[3,3,1,512,128]{4,3,2,1,0:T(8,128)(2,1)}, bf16[3,3,1,512,128]{4,3,2,1,0:T(8,128)(2,1)}, u32[]{:S(2)}, u32[]{:S(2)}) %collective-permute-start.4) | collective-permute-done | bytes 1179680 | tf_op jit(solution)/shard_map/ppermute | solution.py:19
  100.7 0.9 fusion.34
  101.6 24.1 %collective-permute-done.5 = bf16[3,3,1,512,128]{4,3,2,1,0:T(8,128)(2,1)} collective-permute-done((bf16[3,3,1,512,128]{4,3,2,1,0:T(8,128)(2,1)}, bf16[3,3,1,512,128]{4,3,2,1,0:T(8,128)(2,1)}, u32[]{:S(2)}, u32[]{:S(2)}) %collective-permute-start.5) | collective-permute-done | bytes 1179680 | tf_op jit(solution)/shard_map/ppermute | solution.py:21
  125.7 0.9 fusion.33
  126.6 12.1 %gather_fusion = bf16[4096,128]{1,0:T(8,128)(2,1)S(1)} fusion(bf16[4096,128]{1,0:T(8,128)(2,1)S(1)} %fusion.33, s32[4096]{0:T(1024)S(1)} %broadcast_clamp_fusion), kind=kCustom, calls=%fused_computation | custom fusion | bytes 2113536 | tf_op jit(solution)/shard_map/jit(_take)/gather | solution.py:115
  138.7 0.4 add.85
  139.1 0.5 copy-done.8
  139.6 2.6 %multiply_convert_fusion = bf16[4096,128]{1,0:T(8,128)(2,1)S(1)} fusion(f32[4096,128]{1,0:T(8,128)S(1)} %bitcast.52, bf16[4096,128]{1,0:T(8,128)(2,1)S(1)} %gather_fusion, pred[4096]{0:T(1024)(128)(4,1)S(1)} %compare_and_fusion, bf16[256,128]{1,0:T(8,128)(2,1)S(1)} %copy-done.8), kind=kOutput, calls=%fused_computation.17 | convolution fusion | flops 137887744 | bytes 4231168 | tf_op jit(solution)/shard_map/dot_general | solution.py:118
  142.2 0.4 convolution_reduce_fusion
  142.7 0.2 convolution_add_fusion.3
  142.9 0.4 copy-done.3
  143.2 0.3 convolution_add_fusion.2
  143.5 0.0 copy-start.2
  143.6 0.6 multiply_convert_fusion.1
  144.1 0.3 fusion.50
  144.4 0.1 multiply_reduce_fusion.3
  144.5 0.1 add_convert_fusion
  144.7 0.8 copy.15
  (38 shorter events, 0.3 us)
Async XLA Ops:
  0.0 4.1 %copy-start = (bf16[256,128]{1,0:T(8,128)(2,1)S(1)}, bf16[256,128]{1,0:T(8,128)(2,1)}, u32[]{:S(2)}) copy-start(bf16[256,128]{1,0:T(8,128)(2,1)} %param.12) | copy-start | bytes 196612
  0.0 51.4 %copy-start.1 = (bf16[1024,128]{1,0:T(8,128)(2,1)S(1)}, bf16[1024,128]{1,0:T(8,128)(2,1)}, u32[]{:S(2)}) copy-start(bf16[1024,128]{1,0:T(8,128)(2,1)} %param.11) | copy-start | bytes 786436
  0.0 51.3 %copy-start.5 = (s32[32,128]{1,0:T(8,128)S(1)}, s32[32,128]{1,0:T(8,128)}, u32[]{:S(2)}) copy-start(s32[32,128]{1,0:T(8,128)} %param.13) | copy-start | bytes 49156
  0.0 51.4 %copy-start.7 = (bf16[256,128]{1,0:T(8,128)(2,1)S(1)}, bf16[256,128]{1,0:T(8,128)(2,1)}, u32[]{:S(2)}) copy-start(bf16[256,128]{1,0:T(8,128)(2,1)} %param.17) | copy-start | bytes 196612
  1.0 56.8 %collective-permute-start = (bf16[1,1,1,512,128]{4,3,2,1,0:T(8,128)(2,1)S(1)}, bf16[1,1,1,512,128]{4,3,2,1,0:T(8,128)(2,1)S(1)}, u32[]{:S(2)}, u32[]{:S(2)}) collective-permute-start(bf16[1,1,1,512,128]{4,3,2,1,0:T(8,128)(2,1)S(1)} %slice_bitcast_fusion.4), channel_id=1, source_target_pairs={{0,16},{16,0},{1,17},{17,1},{2,18},{18,2},{3,19},{19,3},{4,20},{20... | collective-permute-start | bytes 393224 | tf_op jit(solution)/shard_map/ppermute | solution.py:19
  4.1 53.7 %collective-permute-start.1 = (bf16[1,1,1,512,128]{4,3,2,1,0:T(8,128)(2,1)S(1)}, bf16[1,1,1,512,128]{4,3,2,1,0:T(8,128)(2,1)S(1)}, u32[]{:S(2)}, u32[]{:S(2)}) collective-permute-start(bf16[1,1,1,512,128]{4,3,2,1,0:T(8,128)(2,1)S(1)} %slice_bitcast_fusion.4), channel_id=1, source_target_pairs={{16,0},{0,16},{17,1},{1,17},{18,2},{2,18},{19,3},{3,19},{20,4},{4,... | collective-permute-start | bytes 393224 | tf_op jit(solution)/shard_map/ppermute | solution.py:21
  57.8 9.7 %collective-permute-start.2 = (bf16[3,1,1,512,128]{4,3,2,1,0:T(8,128)(2,1)S(1)}, bf16[3,1,1,512,128]{4,3,2,1,0:T(8,128)(2,1)S(1)}, u32[]{:S(2)}, u32[]{:S(2)}) collective-permute-start(bf16[3,1,1,512,128]{4,3,2,1,0:T(8,128)(2,1)S(1)} %pad_maximum_fusion.1), channel_id=1, source_target_pairs={{0,4},{4,8},{8,12},{12,0},{1,5},{5,9},{9,13},{13,1},{2,6},{6,10},{... | collective-permute-start | bytes 1179656 | tf_op jit(solution)/shard_map/ppermute | solution.py:19
  57.9 10.4 %collective-permute-start.3 = (bf16[3,1,1,512,128]{4,3,2,1,0:T(8,128)(2,1)S(1)}, bf16[3,1,1,512,128]{4,3,2,1,0:T(8,128)(2,1)S(1)}, u32[]{:S(2)}, u32[]{:S(2)}) collective-permute-start(bf16[3,1,1,512,128]{4,3,2,1,0:T(8,128)(2,1)S(1)} %pad_maximum_fusion.1), channel_id=1, source_target_pairs={{4,0},{8,4},{12,8},{0,12},{5,1},{9,5},{13,9},{1,13},{6,2},{10,6},{... | collective-permute-start | bytes 1179656 | tf_op jit(solution)/shard_map/ppermute | solution.py:21
  69.4 31.2 %collective-permute-start.4 = (bf16[3,3,1,512,128]{4,3,2,1,0:T(8,128)(2,1)}, bf16[3,3,1,512,128]{4,3,2,1,0:T(8,128)(2,1)}, u32[]{:S(2)}, u32[]{:S(2)}) collective-permute-start(bf16[3,3,1,512,128]{4,3,2,1,0:T(8,128)(2,1)} %pad_maximum_fusion), channel_id=1, source_target_pairs={{0,1},{1,2},{2,3},{3,0},{4,5},{5,6},{6,7},{7,4},{8,9},{9,10},{10,1... | collective-permute-start | bytes 3538952 | tf_op jit(solution)/shard_map/ppermute | solution.py:19
  71.7 54.0 %collective-permute-start.5 = (bf16[3,3,1,512,128]{4,3,2,1,0:T(8,128)(2,1)}, bf16[3,3,1,512,128]{4,3,2,1,0:T(8,128)(2,1)}, u32[]{:S(2)}, u32[]{:S(2)}) collective-permute-start(bf16[3,3,1,512,128]{4,3,2,1,0:T(8,128)(2,1)} %pad_maximum_fusion), channel_id=1, source_target_pairs={{1,0},{2,1},{3,2},{0,3},{5,4},{6,5},{7,6},{4,7},{9,8},{10,9},{11,1... | collective-permute-start | bytes 3538952 | tf_op jit(solution)/shard_map/ppermute | solution.py:21
  138.7 0.8 copy-start.8
  139.6 2.6 %copy-start.10 = (bf16[128,128]{1,0:T(8,128)(2,1)S(1)}, bf16[128,128]{1,0:T(8,128)(2,1)}, u32[]{:S(2)}) copy-start(bf16[128,128]{1,0:T(8,128)(2,1)} %param.18) | copy-start | bytes 98308
  139.6 3.1 %copy-start.4 = (bf16[512,128]{1,0:T(8,128)(2,1)S(1)}, bf16[512,128]{1,0:T(8,128)(2,1)}, u32[]{:S(2)}) copy-start(bf16[512,128]{1,0:T(8,128)(2,1)} %param.19) | copy-start | bytes 393220
  142.2 1.0 copy-start.3
  142.2 1.3 copy-start.11
  143.2 0.9 copy-start.6
  143.5 1.0 copy-start.2
  143.5 1.0 copy-start.9
where the time goes:
time: 146 us
  waiting for transfers between devices  52.3 us (36%)
  blocking collectives  50.3 us (34%)
  local copies, waits for them, and re-layouts  18 us (12%)
  matrix products  12.3 us (8%)
  starting transfers between devices  9.03 us (6%)
  other arithmetic  3.29 us (2%)
    ppermute x3, waiting for transfers between devices, extended_2(): lax.ppermute(tail, axis, [(i, (i + 1) % count) for i in range(count)])  27.4 us
    ppermute x3, waiting for transfers between devices, extended_2(): lax.ppermute(head, axis, [((i + 1) % count, i) for i in range(count)])  24.9 us
    all_gather x1, blocking collectives, on_device(): lax.all_gather(value_rows, 'gz', axis=0, tiled=True)  14.4 us
    all_gather x1, blocking collectives, on_device(): lax.all_gather(key_rows, 'gz', axis=0, tiled=True)  14.1 us
    gather x1, local copies, waits for them, and re-layouts, on_device(): sender_rows = jnp.take(extended, senders.reshape(-1), axis=0)  12.1 us
    all_gather x1, blocking collectives, on_device(): lax.all_gather(key_rows, 'gy', axis=0, tiled=True)  6.17 us
    all_gather x1, blocking collectives, on_device(): lax.all_gather(value_rows, 'gy', axis=0, tiled=True)  5.78 us
    ppermute x3, starting transfers between devices, extended_2(): lax.ppermute(tail, axis, [(i, (i + 1) % count) for i in range(count)])  5.33 us
  transfers between devices with their start and end apart: 6, of which 4 were waited for; matrix products, arithmetic and copies ran while one was open for 8% of the time, Pallas kernels for 0%

commit v1 on v0

v1 whole, which is shorter than its diff:
```python
import functools
import math

import jax
import jax.numpy as jnp
from jax import lax
from jax.experimental import pallas as pl
from jax.experimental.pallas import tpu as pltpu
from jax.sharding import PartitionSpec as P

BND = 512
AXES = ("gx", "gy", "gz")
F32 = jnp.float32
BF16 = jnp.bfloat16
TILE = 128


def mm(a, b):
    return jnp.dot(a, b, preferred_element_type=F32)


def silu(x):
    h = 0.5 * x
    return h + h * jnp.tanh(h)


def kernel(sizes, *refs):
    (node_h, clus_h, send_h, memb_h, wk_h, wv_h, wei_h, weo_h, wni_h, wno_h, gain_h) = refs[:11]
    out_ref = refs[11]
    (node, clus, send, memb, wk, wv, wei, weo, wni, wno, gain) = refs[12:23]
    rc = refs[23:26]
    rb = refs[26]
    kk, vv = refs[27], refs[28]
    table, rcv, gat, o_own, m_own, pooled = refs[29:35]
    loc_sem, cs_sem, cr_sem, bs_sem, br_sem = refs[35:40]

    count, width = node.shape
    ncl = clus.shape[0]
    deg = send.shape[0] * send.shape[1] // count
    c2 = math.log2(math.e) / math.sqrt(width)
    me = [lax.axis_index(a) for a in AXES]

    def at(axis, off):
        coords = list(me)
        coords[axis] = lax.rem(me[axis] + off, sizes[axis])
        return tuple(coords)

    barrier = pltpu.get_barrier_semaphore()
    greeted = 0
    for axis in range(3):
        for off in range(1, sizes[axis]):
            pl.semaphore_signal(
                barrier, inc=1, device_id=at(axis, off), device_id_type=pl.DeviceIdType.MESH
            )
            greeted += 1

    locals_ = []
    pairs = (
        (clus_h, clus), (wk_h, wk), (wv_h, wv), (node_h, node), (wei_h, wei), (memb_h, memb),
        (send_h, send), (wni_h, wni), (weo_h, weo), (wno_h, wno), (gain_h, gain),
    )
    for i, (src, dst) in enumerate(pairs):
        cp = pltpu.make_async_copy(src, dst, loc_sem.at[i])
        cp.start()
        locals_.append(cp)

    pl.semaphore_wait(barrier, greeted)

    clus_copies = [[], [], []]
    idx = 0
    for axis in (2, 1, 0):
        for off in range(1, sizes[axis]):
            cp = pltpu.make_async_remote_copy(
                src_ref=clus_h,
                dst_ref=rc[axis].at[pl.ds((off - 1) * ncl, ncl)],
                send_sem=cs_sem.at[idx],
                recv_sem=cr_sem.at[idx],
                device_id=at(axis, off),
                device_id_type=pl.DeviceIdType.MESH,
            )
            cp.start()
            clus_copies[axis].append(cp)
            idx += 1
    bnd_copies = {}
    for axis in (2, 1, 0):
        n = sizes[axis]
        for side, off in ((0, 1), (1, n - 1)):
            if side == 1 and n == 2:
                continue
            slot = 2 * axis + side
            cp = pltpu.make_async_remote_copy(
                src_ref=node_h.at[pl.ds(0, BND)],
                dst_ref=rb.at[slot],
                send_sem=bs_sem.at[slot],
                recv_sem=br_sem.at[slot],
                device_id=at(axis, off),
                device_id_type=pl.DeviceIdType.MESH,
            )
            cp.start()
            bnd_copies[slot] = cp

    for cp in locals_:
        cp.wait()

    ones = jnp.ones((ncl, width), BF16)

    def put_kv(rows, base):
        kk[pl.ds(base, ncl), :] = mm(rows, wk[...]).astype(BF16)
        vv[pl.ds(base, ncl), pl.ds(0, width)] = mm(rows, wv[...]).astype(BF16)
        vv[pl.ds(base, ncl), pl.ds(width, width)] = ones

    def attend(q, base, n):
        s = lax.dot_general(
            q, kk[pl.ds(base, n), :], (((1,), (1,)), ((), ())), preferred_element_type=F32
        )
        m = jnp.max(s, axis=1, keepdims=True)
        e = jnp.exp2((s - m) * c2).astype(BF16)
        return m, mm(e, vv[pl.ds(base, n), :])

    tiles = count // TILE

    put_kv(clus[...], 0)

    def first(t, carry):
        rows = pl.ds(pl.multiple_of(t * TILE, TILE), TILE)
        q = node[rows, :]
        table[rows, :] = mm(q, wei[pl.ds(width, width), :])
        rcv[rows, :] = mm(q, wei[pl.ds(0, width), :])
        m, o = attend(q, 0, ncl)
        m_own[rows, :] = jnp.broadcast_to(m, (TILE, width))
        o_own[rows, :] = o
        return carry

    lax.fori_loop(0, tiles, first, 0)

    base = ncl
    spans = []
    for axis in range(3):
        spans.append((base, (sizes[axis] - 1) * ncl))
        base += (sizes[axis] - 1) * ncl
    for axis in (2, 1, 0):
        for j, cp in enumerate(clus_copies[axis]):
            cp.wait_recv()
            put_kv(rc[axis][pl.ds(j * ncl, ncl), :], spans[axis][0] + j * ncl)

    def lines(t, carry):
        rows = pl.ds(pl.multiple_of(t * TILE, TILE), TILE)
        q = node[rows, :]
        m0 = m_own[rows, :]
        n0 = o_own[rows, pl.ds(0, width)]
        d0 = o_own[rows, pl.ds(width, width)]
        total = jnp.zeros((TILE, width), F32)
        for axis in range(3):
            m1, o1 = attend(q, *spans[axis])
            top = jnp.maximum(m0, m1)
            a0 = jnp.exp2((m0 - top) * c2)
            a1 = jnp.exp2((m1 - top) * c2)
            numer = a0 * n0 + a1 * o1[:, :width]
            denom = a0 * d0 + a1 * o1[:, width:]
            total = total + numer / denom
        att = total * lax.rsqrt(jnp.mean(total * total, axis=1, keepdims=True) + 1e-6)
        pooled[rows, :] = att.astype(BF16)
        return carry

    lax.fori_loop(0, tiles, lines, 0)

    for axis in (2, 1, 0):
        for side in range(2):
            slot = 2 * axis + side
            if slot not in bnd_copies:
                continue
            bnd_copies[slot].wait_recv()
            proj = mm(rb[slot], wei[pl.ds(width, width), :])
            table[pl.ds(count + slot * BND, BND), :] = proj
            if sizes[axis] == 2:
                table[pl.ds(count + (slot + 1) * BND, BND), :] = proj

    lane_rows = TILE * deg // send.shape[1]

    def gather(g, carry):
        for c in range(send.shape[1]):
            s = send[g, c]
            dst = g * (send.shape[1] // deg) + c // deg
            gat[c % deg, pl.ds(dst, 1), :] = table[pl.ds(s, 1), :]
        return carry

    lax.fori_loop(0, send.shape[0], gather, 0)

    cluster_ids = lax.broadcasted_iota(jnp.int32, (TILE, ncl), 1)

    def last(t, carry):
        rows = pl.ds(pl.multiple_of(t * TILE, TILE), TILE)
        q = node[rows, :]
        r = rcv[rows, :]
        hidden = silu(gat[0, rows, :] + r)
        for d in range(1, deg):
            hidden = hidden + silu(gat[d, rows, :] + r)
        agg = mm(hidden.astype(BF16), weo[...]).astype(BF16)
        ids = jnp.broadcast_to(memb[pl.ds(t, 1), :], (TILE, TILE)).T[:, :1]
        hot = jnp.where(cluster_ids == ids, 1.0, 0.0).astype(BF16)
        own = mm(hot, clus[...]).astype(BF16)
        pre = mm(jnp.concatenate([q, agg, pooled[rows, :], own], axis=1), wni[...])
        update = mm(silu(pre).astype(BF16), wno[...])
        cen = update - jnp.mean(update, axis=1, keepdims=True)
        var = jnp.mean(cen * cen, axis=1, keepdims=True)
        normed = cen * lax.rsqrt(var + 1e-5)
        out_ref[rows, :] = (q.astype(F32) + normed * gain[...]).astype(BF16)
        return carry

    lax.fori_loop(0, tiles, last, 0)

    for group in clus_copies:
        for cp in group:
            cp.wait_send()
    for cp in bnd_copies.values():
        cp.wait_send()


def solution(mesh):
    sizes = tuple(mesh.shape[a] for a in AXES)

    def on_device(node, clus, send, memb, wk, wv, wei, weo, wni, wno, gain):
        count, width = node.shape
        ncl = clus.shape[0]
        deg = send.size // count
        memb = memb.reshape(count // TILE, TILE)
        gain = gain.reshape(1, width)
        args = (node, clus, send, memb, wk, wv, wei, weo, wni, wno, gain)
        peers = sum(n - 1 for n in sizes)
        total = ncl * (1 + peers)
        scratch = []
        for i, a in enumerate(args):
            space = pltpu.SMEM if i == 2 else pltpu.VMEM
            scratch.append(space(a.shape, a.dtype))
        scratch += [pltpu.VMEM(((n - 1) * ncl, width), BF16) for n in sizes]
        scratch += [
            pltpu.VMEM((6, BND, width), BF16),
            pltpu.VMEM((total, width), BF16),
            pltpu.VMEM((total, 2 * width), BF16),
            pltpu.VMEM((count + 6 * BND, width), F32),
            pltpu.VMEM((count, width), F32),
            pltpu.VMEM((deg, count, width), F32),
            pltpu.VMEM((count, 2 * width), F32),
            pltpu.VMEM((count, width), F32),
            pltpu.VMEM((count, width), BF16),
            pltpu.SemaphoreType.DMA((len(args),)),
            pltpu.SemaphoreType.DMA((peers,)),
            pltpu.SemaphoreType.DMA((peers,)),
            pltpu.SemaphoreType.DMA((6,)),
            pltpu.SemaphoreType.DMA((6,)),
        ]
        return pl.pallas_call(
            functools.partial(kernel, sizes),
            out_shape=jax.ShapeDtypeStruct((count, width), BF16),
            in_specs=[pl.BlockSpec(memory_space=pl.ANY)] * len(args),
            out_specs=pl.BlockSpec(memory_space=pltpu.VMEM),
            scratch_shapes=scratch,
            compiler_params=pltpu.CompilerParams(
                collective_id=0, has_side_effects=True, vmem_limit_bytes=48 * 1024 * 1024
            ),
        )(*args)

    spec = P(AXES, None)
    return jax.shard_map(
        on_device,
        mesh=mesh,
        in_specs=(spec, spec, spec, P(AXES)) + (P(),) * 7,
        out_specs=spec,
        check_vma=False,
    )
```

time: 146 us -> 42 us (0.29)
  the two profiles are of different devices: /device:TPU:0 before, /device:TPU:8 now
where the time goes in v1:
time: 42 us; the launch traced here: 41.3 us
  Pallas kernels  32 us (76%)
  local copies, waits for them, and re-layouts  9.32 us (22%)
    pallas_call x1, Pallas kernels, on_device(): pl.pallas_call(functools.partial(kernel, sizes), out_shape=jax.ShapeDtype...  32 us
    unnamed x23, local copies, waits for them, and re-layouts  9.32 us

profile of v1, /device:TPU:8, one launch (start us, length us, event | category | flops | bytes accessed | tf_op | source)
XLA Modules:
  0.0 41.3 jit_solution(10179898163668331764)
XLA Ops:
  0.0 0.0 copy-start.10
  0.0 0.7 %copy-done.10 = f32[128]{0:T(128)S(1)} copy-done((f32[128]{0:T(128)S(1)}, f32[128]{0:T(128)}, u32[]{:S(2)}) %copy-start.10) | copy-done | bytes 536
  0.7 0.0 copy-start
  0.7 0.9 %copy-done = bf16[1024,128]{1,0:T(8,128)(2,1)S(1)} copy-done((bf16[1024,128]{1,0:T(8,128)(2,1)S(1)}, bf16[1024,128]{1,0:T(8,128)(2,1)}, u32[]{:S(2)}) %copy-start) | copy-done | bytes 262168
  1.6 0.0 copy-start.1
  1.6 0.9 %copy-done.1 = bf16[512,128]{1,0:T(8,128)(2,1)S(1)} copy-done((bf16[512,128]{1,0:T(8,128)(2,1)S(1)}, bf16[512,128]{1,0:T(8,128)(2,1)}, u32[]{:S(2)}) %copy-start.1) | copy-done | bytes 131096
  2.5 0.0 copy-start.2
  2.5 0.8 %copy-done.2 = bf16[256,128]{1,0:T(8,128)(2,1)S(1)} copy-done((bf16[256,128]{1,0:T(8,128)(2,1)S(1)}, bf16[256,128]{1,0:T(8,128)(2,1)}, u32[]{:S(2)}) %copy-start.2) | copy-done | bytes 65560
  3.4 0.0 copy-start.3
  3.4 0.8 %copy-done.3 = bf16[256,128]{1,0:T(8,128)(2,1)S(1)} copy-done((bf16[256,128]{1,0:T(8,128)(2,1)S(1)}, bf16[256,128]{1,0:T(8,128)(2,1)}, u32[]{:S(2)}) %copy-start.3) | copy-done | bytes 65560
  4.2 0.0 copy-start.4
  4.2 0.8 %copy-done.4 = bf16[128,128]{1,0:T(8,128)(2,1)S(1)} copy-done((bf16[128,128]{1,0:T(8,128)(2,1)S(1)}, bf16[128,128]{1,0:T(8,128)(2,1)}, u32[]{:S(2)}) %copy-start.4) | copy-done | bytes 32792
  5.0 0.0 copy-start.5
  5.0 0.8 %copy-done.5 = bf16[128,128]{1,0:T(8,128)(2,1)S(1)} copy-done((bf16[128,128]{1,0:T(8,128)(2,1)S(1)}, bf16[128,128]{1,0:T(8,128)(2,1)}, u32[]{:S(2)}) %copy-start.5) | copy-done | bytes 32792
  5.7 0.0 copy-start.6
  5.7 0.8 %copy-done.6 = bf16[128,128]{1,0:T(8,128)(2,1)S(1)} copy-done((bf16[128,128]{1,0:T(8,128)(2,1)S(1)}, bf16[128,128]{1,0:T(8,128)(2,1)}, u32[]{:S(2)}) %copy-start.6) | copy-done | bytes 32792
  6.5 0.0 copy-start.7
  6.5 0.8 %copy-done.7 = bf16[128,128]{1,0:T(8,128)(2,1)S(1)} copy-done((bf16[128,128]{1,0:T(8,128)(2,1)S(1)}, bf16[128,128]{1,0:T(8,128)(2,1)}, u32[]{:S(2)}) %copy-start.7) | copy-done | bytes 32792
  7.2 0.0 copy-start.8
  7.2 0.7 %copy-done.8 = s32[32,128]{1,0:T(8,128)S(1)} copy-done((s32[32,128]{1,0:T(8,128)S(1)}, s32[32,128]{1,0:T(8,128)}, u32[]{:S(2)}) %copy-start.8) | copy-done | bytes 16408
  7.9 0.0 copy-start.9
  7.9 0.7 %copy-done.9 = s32[1024]{0:T(1024)S(1)} copy-done((s32[1024]{0:T(1024)S(1)}, s32[1024]{0:T(1024)}, u32[]{:S(2)}) %copy-start.9) | copy-done | bytes 4120
  8.6 32.0 %shard_map.109 = bf16[1024,128]{1,0:T(8,128)(2,1)S(1)} custom-call(bf16[1024,128]{1,0:T(8,128)(2,1)S(1)} %copy-done, bf16[256,128]{1,0:T(8,128)(2,1)S(1)} %copy-done.2, s32[32,128]{1,0:T(8,128)S(1)} %copy-done.8, s32[8,128]{1,0:T(8,128)S(1)} %bitcast.2, bf16[128,128]{1,0:T(8,128)(2,1)S(1)} %copy-done.4, bf16[128,128]{1,0:T(8,128)(2,1)S(1)} %copy-done.5, ...), custom_call_target="tpu_custom_call" | custom-call | tf_op jit(solution)/shard_map/pallas_call | solution.py:252
  40.6 0.7 %copy.13 = bf16[1024,128]{1,0:T(8,128)(2,1)} copy(bf16[1024,128]{1,0:T(8,128)(2,1)S(1)} %shard_map.109) | data formatting | bytes 524288
Async XLA Ops:
  0.0 0.7 %copy-start.10 = (f32[128]{0:T(128)S(1)}, f32[128]{0:T(128)}, u32[]{:S(2)}) copy-start(f32[128]{0:T(128)} %param.21) | copy-start | bytes 1540
  0.7 0.9 %copy-start = (bf16[1024,128]{1,0:T(8,128)(2,1)S(1)}, bf16[1024,128]{1,0:T(8,128)(2,1)}, u32[]{:S(2)}) copy-start(bf16[1024,128]{1,0:T(8,128)(2,1)} %refs_0_.1) | copy-start | bytes 786436
  1.6 0.9 %copy-start.1 = (bf16[512,128]{1,0:T(8,128)(2,1)S(1)}, bf16[512,128]{1,0:T(8,128)(2,1)}, u32[]{:S(2)}) copy-start(bf16[512,128]{1,0:T(8,128)(2,1)} %refs_8_.1) | copy-start | bytes 393220
  2.5 0.8 %copy-start.2 = (bf16[256,128]{1,0:T(8,128)(2,1)S(1)}, bf16[256,128]{1,0:T(8,128)(2,1)}, u32[]{:S(2)}) copy-start(bf16[256,128]{1,0:T(8,128)(2,1)} %refs_1_.1) | copy-start | bytes 196612
  3.4 0.8 %copy-start.3 = (bf16[256,128]{1,0:T(8,128)(2,1)S(1)}, bf16[256,128]{1,0:T(8,128)(2,1)}, u32[]{:S(2)}) copy-start(bf16[256,128]{1,0:T(8,128)(2,1)} %refs_6_.1) | copy-start | bytes 196612
  4.2 0.8 %copy-start.4 = (bf16[128,128]{1,0:T(8,128)(2,1)S(1)}, bf16[128,128]{1,0:T(8,128)(2,1)}, u32[]{:S(2)}) copy-start(bf16[128,128]{1,0:T(8,128)(2,1)} %refs_4_.1) | copy-start | bytes 98308
  5.0 0.8 %copy-start.5 = (bf16[128,128]{1,0:T(8,128)(2,1)S(1)}, bf16[128,128]{1,0:T(8,128)(2,1)}, u32[]{:S(2)}) copy-start(bf16[128,128]{1,0:T(8,128)(2,1)} %refs_5_.1) | copy-start | bytes 98308
  5.7 0.8 %copy-start.6 = (bf16[128,128]{1,0:T(8,128)(2,1)S(1)}, bf16[128,128]{1,0:T(8,128)(2,1)}, u32[]{:S(2)}) copy-start(bf16[128,128]{1,0:T(8,128)(2,1)} %refs_7_.1) | copy-start | bytes 98308
  6.5 0.8 %copy-start.7 = (bf16[128,128]{1,0:T(8,128)(2,1)S(1)}, bf16[128,128]{1,0:T(8,128)(2,1)}, u32[]{:S(2)}) copy-start(bf16[128,128]{1,0:T(8,128)(2,1)} %refs_9_.1) | copy-start | bytes 98308
  7.2 0.7 %copy-start.8 = (s32[32,128]{1,0:T(8,128)S(1)}, s32[32,128]{1,0:T(8,128)}, u32[]{:S(2)}) copy-start(s32[32,128]{1,0:T(8,128)} %refs_2_.1) | copy-start | bytes 49156
  7.9 0.7 %copy-start.9 = (s32[1024]{0:T(1024)S(1)}, s32[1024]{0:T(1024)}, u32[]{:S(2)}) copy-start(s32[1024]{0:T(1024)} %param.14) | copy-start | bytes 12292

commit v2 on v1

v2 whole, which is shorter than its diff:
```python
import functools
import math

import jax
import jax.numpy as jnp
from jax import lax
from jax.experimental import pallas as pl
from jax.experimental.pallas import tpu as pltpu
from jax.sharding import PartitionSpec as P

BND = 512
AXES = ("gx", "gy", "gz")
F32 = jnp.float32
BF16 = jnp.bfloat16
TILE = 128
TA = 256
TZ = 256


def mm(a, b):
    return jnp.dot(a, b, preferred_element_type=F32)


def silu(x):
    h = 0.5 * x
    return h + h * jnp.tanh(h)


def kernel(sizes, *refs):
    (node_h, clus_h, send_h, memb_h, wk_h, wv_h, wei_h, weo_h, wni_h, wno_h, gain_h) = refs[:11]
    out_ref = refs[11]
    (node, clus, send, memb, wk, wv, wei, weo, wni, wno, gain) = refs[12:23]
    rc = refs[23:26]
    rb = refs[26]
    kk, vv = refs[27], refs[28]
    table, rcv, gat, o_own, m_own, pooled, pre = refs[29:36]
    loc_sem, cs_sem, cr_sem, bs_sem, br_sem, zs_sem, zr_sem = refs[36:43]

    count, width = node.shape
    ncl = clus.shape[0]
    deg = send.shape[0] * send.shape[1] // count
    c2 = math.log2(math.e) / math.sqrt(width)
    me = [lax.axis_index(a) for a in AXES]

    def at(axis, off):
        coords = list(me)
        coords[axis] = lax.rem(me[axis] + off, sizes[axis])
        return tuple(coords)

    barrier = pltpu.get_barrier_semaphore()
    greeted = 0
    for axis in range(3):
        for off in range(1, sizes[axis]):
            pl.semaphore_signal(
                barrier, inc=1, device_id=at(axis, off), device_id_type=pl.DeviceIdType.MESH
            )
            greeted += 1

    locals_ = []
    pairs = (
        (clus_h, clus), (wk_h, wk), (wv_h, wv), (node_h, node), (wei_h, wei), (memb_h, memb),
        (send_h, send), (wni_h, wni), (weo_h, weo), (wno_h, wno), (gain_h, gain),
    )
    for i, (src, dst) in enumerate(pairs):
        cp = pltpu.make_async_copy(src, dst, loc_sem.at[i])
        cp.start()
        locals_.append(cp)

    with jax.named_scope("p_barrier"):
        pl.semaphore_wait(barrier, greeted)

    zn = sizes[2]
    zi = me[2]

    def remote(src, dst, ssem, rsem, dev):
        return pltpu.make_async_remote_copy(
            src_ref=src, dst_ref=dst, send_sem=ssem, recv_sem=rsem,
            device_id=dev, device_id_type=pl.DeviceIdType.MESH,
        )

    def z_slot(i):
        return rc[2].at[pl.ds(i * ncl, ncl)]

    def hop(step, up):
        i = step if up else zn - 2 - step
        j = step - 1 if up else zn - 1 - step
        src = clus_h if step == 0 else z_slot(j)
        k = 2 * step + (0 if up else 1)
        go = jnp.logical_and(zi >= step, zi < zn - 1) if up else jnp.logical_and(zi < zn - step, zi > 0)
        return go, remote(src, z_slot(i), zs_sem.at[k], zr_sem.at[i], at(2, 1 if up else zn - 1))

    def z_recv(i):
        return remote(clus_h, z_slot(i), zs_sem.at[0], zr_sem.at[i], at(2, 1))

    def start_hop(step):
        for up in (True, False):
            go, cp = hop(step, up)

            @pl.when(go)
            def _():
                if step > 0:
                    z_recv(step - 1 if up else zn - 1 - step).wait_recv()
                cp.start()

    def boundary(axis):
        n = sizes[axis]
        for side, off in ((0, 1), (1, n - 1)):
            if side == 1 and n == 2:
                continue
            slot = 2 * axis + side
            cp = remote(node_h.at[pl.ds(0, BND)], rb.at[slot], bs_sem.at[slot], br_sem.at[slot], at(axis, off))
            cp.start()
            bnd_copies[slot] = cp

    bnd_copies = {}
    clus_copies = [[], []]
    start_hop(0)
    boundary(2)
    idx = 0
    for axis in (0, 1):
        for off in range(1, sizes[axis]):
            cp = remote(
                clus_h, rc[axis].at[pl.ds((off - 1) * ncl, ncl)], cs_sem.at[idx], cr_sem.at[idx], at(axis, off)
            )
            cp.start()
            clus_copies[axis].append(cp)
            idx += 1
    boundary(0)
    boundary(1)

    with jax.named_scope("p_local"):
        for cp in locals_:
            cp.wait()

    ones = jnp.ones((ncl, width), BF16)

    def put_kv(rows, base):
        kk[pl.ds(base, ncl), :] = mm(rows, wk[...]).astype(BF16)
        vv[pl.ds(base, ncl), pl.ds(0, width)] = mm(rows, wv[...]).astype(BF16)
        vv[pl.ds(base, ncl), pl.ds(width, width)] = ones

    def attend(q, base, n):
        s = lax.dot_general(
            q, kk[pl.ds(base, n), :], (((1,), (1,)), ((), ())), preferred_element_type=F32
        )
        m = jnp.max(s, axis=1, keepdims=True)
        e = jnp.exp2((s - m) * c2).astype(BF16)
        return m, mm(e, vv[pl.ds(base, n), :])

    put_kv(clus[...], 0)
    cluster_ids = lax.broadcasted_iota(jnp.int32, (TILE, ncl), 1)

    def first(t, carry):
        rows = pl.ds(pl.multiple_of(t * TA, TA), TA)
        q = node[rows, :]
        table[rows, :] = mm(q, wei[pl.ds(width, width), :])
        rcv[rows, :] = mm(q, wei[pl.ds(0, width), :])
        hots = []
        for j in range(TA // TILE):
            ids = jnp.broadcast_to(memb[pl.ds(t * (TA // TILE) + j, 1), :], (TILE, TILE)).T[:, :1]
            hots.append(jnp.where(cluster_ids == ids, 1.0, 0.0).astype(BF16))
        own = mm(jnp.concatenate(hots, axis=0), clus[...]).astype(BF16)
        pre[rows, :] = mm(q, wni[pl.ds(0, width), :]) + mm(own, wni[pl.ds(3 * width, width), :])
        m, o = attend(q, 0, ncl)
        m_own[rows, :] = jnp.broadcast_to(m, (TA, width))
        o_own[rows, :] = o
        return carry

    with jax.named_scope("p_first"):
        lax.fori_loop(0, count // TA, first, 0)

    for step in range(1, min(2, zn - 1)):
        with jax.named_scope("p_hop1"):
            start_hop(step)

    base = ncl
    spans = []
    for axis in range(3):
        spans.append((base, (sizes[axis] - 1) * ncl))
        base += (sizes[axis] - 1) * ncl
    for axis in (0, 1):
        for j, cp in enumerate(clus_copies[axis]):
            with jax.named_scope("p_wkv"):
                cp.wait_recv()
            put_kv(rc[axis][pl.ds(j * ncl, ncl), :], spans[axis][0] + j * ncl)

    def line(q, rows, axis):
        m0 = m_own[rows, :]
        n0 = o_own[rows, pl.ds(0, width)]
        d0 = o_own[rows, pl.ds(width, width)]
        m1, o1 = attend(q, *spans[axis])
        top = jnp.maximum(m0, m1)
        a0 = jnp.exp2((m0 - top) * c2)
        a1 = jnp.exp2((m1 - top) * c2)
        numer = a0 * n0 + a1 * o1[:, :width]
        denom = a0 * d0 + a1 * o1[:, width:]
        return numer / denom

    def lines(t, carry):
        rows = pl.ds(pl.multiple_of(t * TA, TA), TA)
        q = node[rows, :]
        pooled[rows, :] = line(q, rows, 0) + line(q, rows, 1)
        return carry

    with jax.named_scope("p_lines"):
        lax.fori_loop(0, count // TA, lines, 0)

    for step in range(2, zn - 1):
        with jax.named_scope("p_hop2"):
            start_hop(step)

    for axis in (0, 1, 2):
        for side in range(2):
            slot = 2 * axis + side
            if slot not in bnd_copies:
                continue
            with jax.named_scope("p_wb"):
                bnd_copies[slot].wait_recv()
            proj = mm(rb[slot], wei[pl.ds(width, width), :])
            table[pl.ds(count + slot * BND, BND), :] = proj
            if sizes[axis] == 2:
                table[pl.ds(count + (slot + 1) * BND, BND), :] = proj

    lanes = send.shape[1]
    per = TILE * deg // lanes

    def gather(t):
        for g in range(per):
            for c in range(lanes):
                s = send[t * per + g, c]
                dst = t * TILE + (g * lanes + c) // deg
                gat[c % deg, pl.ds(dst, 1), :] = table[pl.ds(s, 1), :]

    def edges(t):
        rows = pl.ds(pl.multiple_of(t * TILE, TILE), TILE)
        r = rcv[rows, :]
        hidden = silu(gat[0, rows, :] + r)
        for d in range(1, deg):
            hidden = hidden + silu(gat[d, rows, :] + r)
        agg = mm(hidden.astype(BF16), weo[...]).astype(BF16)
        pre[rows, :] = pre[rows, :] + mm(agg, wni[pl.ds(width, width), :])

    def edge_step(t, carry):
        edges(t - 1)
        gather(t)
        return carry

    with jax.named_scope("p_gather"):
        gather(0)
        lax.fori_loop(1, count // TILE, edge_step, 0)
        edges(count // TILE - 1)

    for j in range(zn - 1):
        with jax.named_scope("p_wz"):
            passed = jnp.logical_or(
                jnp.logical_and(j < zi, jnp.logical_and(zi < zn - 1, j < zn - 2)),
                jnp.logical_and(j >= zi, jnp.logical_and(zi > 0, j > 0)),
            )

            @pl.when(jnp.logical_not(passed))
            def _():
                z_recv(j).wait_recv()
        put_kv(rc[2][pl.ds(j * ncl, ncl), :], spans[2][0] + j * ncl)

    def last(t, carry):
        rows = pl.ds(pl.multiple_of(t * TZ, TZ), TZ)
        q = node[rows, :]
        total = pooled[rows, :] + line(q, rows, 2)
        att = total * lax.rsqrt(jnp.mean(total * total, axis=1, keepdims=True) + 1e-6)
        p = pre[rows, :] + mm(att.astype(BF16), wni[pl.ds(2 * width, width), :])
        update = mm(silu(p).astype(BF16), wno[...])
        cen = update - jnp.mean(update, axis=1, keepdims=True)
        var = jnp.mean(cen * cen, axis=1, keepdims=True)
        normed = cen * lax.rsqrt(var + 1e-5)
        out_ref[rows, :] = (q.astype(F32) + normed * gain[...]).astype(BF16)
        return carry

    with jax.named_scope("p_last"):
        lax.fori_loop(0, count // TZ, last, 0)

    for group in clus_copies:
        for cp in group:
            cp.wait_send()
    for cp in bnd_copies.values():
        cp.wait_send()
    for step in range(zn - 1):
        for up in (True, False):
            go, cp = hop(step, up)

            @pl.when(go)
            def _():
                cp.wait_send()


def solution(mesh):
    sizes = tuple(mesh.shape[a] for a in AXES)

    def on_device(node, clus, send, memb, wk, wv, wei, weo, wni, wno, gain):
        count, width = node.shape
        ncl = clus.shape[0]
        deg = send.size // count
        memb = memb.reshape(count // TILE, TILE)
        gain = gain.reshape(1, width)
        args = (node, clus, send, memb, wk, wv, wei, weo, wni, wno, gain)
        peers = sum(n - 1 for n in sizes)
        total = ncl * (1 + peers)
        scratch = []
        for i, a in enumerate(args):
            space = pltpu.SMEM if i == 2 else pltpu.VMEM
            scratch.append(space(a.shape, a.dtype))
        scratch += [pltpu.VMEM(((n - 1) * ncl, width), BF16) for n in sizes]
        scratch += [
            pltpu.VMEM((6, BND, width), BF16),
            pltpu.VMEM((total, width), BF16),
            pltpu.VMEM((total, 2 * width), BF16),
            pltpu.VMEM((count + 6 * BND, width), F32),
            pltpu.VMEM((count, width), F32),
            pltpu.VMEM((deg, count, width), F32),
            pltpu.VMEM((count, 2 * width), F32),
            pltpu.VMEM((count, width), F32),
            pltpu.VMEM((count, width), F32),
            pltpu.VMEM((count, width), F32),
            pltpu.SemaphoreType.DMA((len(args),)),
            pltpu.SemaphoreType.DMA((peers,)),
            pltpu.SemaphoreType.DMA((peers,)),
            pltpu.SemaphoreType.DMA((6,)),
            pltpu.SemaphoreType.DMA((6,)),
            pltpu.SemaphoreType.DMA((2 * sizes[2],)),
            pltpu.SemaphoreType.DMA((sizes[2],)),
        ]
        return pl.pallas_call(
            functools.partial(kernel, sizes),
            out_shape=jax.ShapeDtypeStruct((count, width), BF16),
            in_specs=[pl.BlockSpec(memory_space=pltpu.HBM)] * len(args),
            out_specs=pl.BlockSpec(memory_space=pltpu.VMEM),
            scratch_shapes=scratch,
            compiler_params=pltpu.CompilerParams(
                collective_id=0, has_side_effects=True
            ),
        )(*args)

    spec = P(AXES, None)
    return jax.shard_map(
        on_device,
        mesh=mesh,
        in_specs=(spec, spec, spec, P(AXES)) + (P(),) * 7,
        out_specs=spec,
        check_vma=False,
    )
```

time: 42 us -> 27.3 us (0.65)
  the two profiles are of different devices: /device:TPU:8 before, /device:TPU:1 now
where the time goes in v2:
time: 27.3 us; the launch traced here: 27.2 us
  Pallas kernels  25.5 us (93%)
  local copies, waits for them, and re-layouts  1.67 us (6%)
    pallas_call x1, Pallas kernels, on_device(): pl.pallas_call(functools.partial(kernel, sizes), out_shape=jax.ShapeDtype...  25.5 us
    unnamed x1, local copies, waits for them, and re-layouts  1.67 us

profile of v2, /device:TPU:1, one launch (start us, length us, event | category | flops | bytes accessed | tf_op | source)
XLA Modules:
  0.0 27.2 jit_solution(7248676607997561041)
XLA Ops:
  0.0 25.5 %shard_map.109 = bf16[1024,128]{1,0:T(8,128)(2,1)} custom-call(bf16[1024,128]{1,0:T(8,128)(2,1)} %refs_0_.1, bf16[256,128]{1,0:T(8,128)(2,1)} %refs_1_.1, s32[32,128]{1,0:T(8,128)} %refs_2_.1, s32[8,128]{1,0:T(8,128)} %bitcast.2, bf16[128,128]{1,0:T(8,128)(2,1)} %refs_4_.1, bf16[128,128]{1,0:T(8,128)(2,1)} %refs_5_.1, bf16[256,128]{1,0:T(8,128)(2,1)} %refs_6_.1, ...), custom_call_target="tpu_custom_call" | custom-call | tf_op jit(solution)/shard_map/pallas_call | solution.py:331
  25.5 1.7 %copy.13 = bf16[1024,128]{1,0:T(8,128)(2,1)} copy(bf16[1024,128]{1,0:T(8,128)(2,1)} %shard_map.109) | data formatting | bytes 524288

commit v3 on v2

--- a/solution.py
+++ b/solution.py
@@ -13,8 +13,8 @@
 F32 = jnp.float32
 BF16 = jnp.bfloat16
 TILE = 128
-TA = 256
-TZ = 256
+TA = 512
+TZ = 512
 
 
 def mm(a, b):
@@ -65,6 +65,8 @@
         cp = pltpu.make_async_copy(src, dst, loc_sem.at[i])
         cp.start()
         locals_.append(cp)
+
+    vv[:, pl.ds(width, width)] = jnp.ones((vv.shape[0], width), BF16)
 
     with jax.named_scope("p_barrier"):
         pl.semaphore_wait(barrier, greeted)
@@ -132,17 +134,15 @@
         for cp in locals_:
             cp.wait()
 
-    ones = jnp.ones((ncl, width), BF16)
-
     def put_kv(rows, base):
-        kk[pl.ds(base, ncl), :] = mm(rows, wk[...]).astype(BF16)
-        vv[pl.ds(base, ncl), pl.ds(0, width)] = mm(rows, wv[...]).astype(BF16)
-        vv[pl.ds(base, ncl), pl.ds(width, width)] = ones
-
-    def attend(q, base, n):
-        s = lax.dot_general(
-            q, kk[pl.ds(base, n), :], (((1,), (1,)), ((), ())), preferred_element_type=F32
-        )
+        n = rows.shape[0]
+        kk[:, pl.ds(base, n)] = mm(rows, wk[...]).T.astype(BF16)
+        vv[pl.ds(base, n), pl.ds(0, width)] = mm(rows, wv[...]).astype(BF16)
+
+    def score(q, base, n):
+        return mm(q, kk[:, pl.ds(base, n)])
+
+    def weigh(s, base, n):
         m = jnp.max(s, axis=1, keepdims=True)
         e = jnp.exp2((s - m) * c2).astype(BF16)
         return m, mm(e, vv[pl.ds(base, n), :])
@@ -150,8 +150,8 @@
     put_kv(clus[...], 0)
     cluster_ids = lax.broadcasted_iota(jnp.int32, (TILE, ncl), 1)
 
-    def first(t, carry):
-        rows = pl.ds(pl.multiple_of(t * TA, TA), TA)
+    def first(t):
+        rows = pl.ds(t * TA, TA)
         q = node[rows, :]
         table[rows, :] = mm(q, wei[pl.ds(width, width), :])
         rcv[rows, :] = mm(q, wei[pl.ds(0, width), :])
@@ -161,13 +161,13 @@
             hots.append(jnp.where(cluster_ids == ids, 1.0, 0.0).astype(BF16))
         own = mm(jnp.concatenate(hots, axis=0), clus[...]).astype(BF16)
         pre[rows, :] = mm(q, wni[pl.ds(0, width), :]) + mm(own, wni[pl.ds(3 * width, width), :])
-        m, o = attend(q, 0, ncl)
+        m, o = weigh(score(q, 0, ncl), 0, ncl)
         m_own[rows, :] = jnp.broadcast_to(m, (TA, width))
         o_own[rows, :] = o
-        return carry
 
     with jax.named_scope("p_first"):
-        lax.fori_loop(0, count // TA, first, 0)
+        for t in range(count // TA):
+            first(t)
 
     for step in range(1, min(2, zn - 1)):
         with jax.named_scope("p_hop1"):
@@ -178,17 +178,18 @@
     for axis in range(3):
         spans.append((base, (sizes[axis] - 1) * ncl))
         base += (sizes[axis] - 1) * ncl
+    with jax.named_scope("p_wkv"):
+        for axis in (0, 1):
+            for cp in clus_copies[axis]:
+                cp.wait_recv()
     for axis in (0, 1):
-        for j, cp in enumerate(clus_copies[axis]):
-            with jax.named_scope("p_wkv"):
-                cp.wait_recv()
-            put_kv(rc[axis][pl.ds(j * ncl, ncl), :], spans[axis][0] + j * ncl)
-
-    def line(q, rows, axis):
+        put_kv(rc[axis][...], spans[axis][0])
+
+    def line(s, rows, axis):
         m0 = m_own[rows, :]
         n0 = o_own[rows, pl.ds(0, width)]
         d0 = o_own[rows, pl.ds(width, width)]
-        m1, o1 = attend(q, *spans[axis])
+        m1, o1 = weigh(s, *spans[axis])
         top = jnp.maximum(m0, m1)
         a0 = jnp.exp2((m0 - top) * c2)
         a1 = jnp.exp2((m1 - top) * c2)
@@ -196,30 +197,37 @@
         denom = a0 * d0 + a1 * o1[:, width:]
         return numer / denom
 
-    def lines(t, carry):
-        rows = pl.ds(pl.multiple_of(t * TA, TA), TA)
+    def pipeline(size, ready, use):
+        spots = [pl.ds(i, size) for i in range(0, count, size)]
+        ahead = ready(spots[0])
+        for i, rows in enumerate(spots):
+            now = ahead
+            if i + 1 < len(spots):
+                ahead = ready(spots[i + 1])
+            use(rows, now)
+
+    def lines_ready(rows):
         q = node[rows, :]
-        pooled[rows, :] = line(q, rows, 0) + line(q, rows, 1)
-        return carry
+        return score(q, *spans[0]), score(q, *spans[1])
+
+    def lines_use(rows, now):
+        pooled[rows, :] = line(now[0], rows, 0) + line(now[1], rows, 1)
 
     with jax.named_scope("p_lines"):
-        lax.fori_loop(0, count // TA, lines, 0)
+        pipeline(TA, lines_ready, lines_use)
 
     for step in range(2, zn - 1):
         with jax.named_scope("p_hop2"):
             start_hop(step)
 
-    for axis in (0, 1, 2):
-        for side in range(2):
-            slot = 2 * axis + side
-            if slot not in bnd_copies:
-                continue
-            with jax.named_scope("p_wb"):
-                bnd_copies[slot].wait_recv()
-            proj = mm(rb[slot], wei[pl.ds(width, width), :])
-            table[pl.ds(count + slot * BND, BND), :] = proj
-            if sizes[axis] == 2:
-                table[pl.ds(count + (slot + 1) * BND, BND), :] = proj
+    with jax.named_scope("p_wb"):
+        for cp in bnd_copies.values():
+            cp.wait_recv()
+    for slot in bnd_copies:
+        proj = mm(rb[slot], wei[pl.ds(width, width), :])
+        table[pl.ds(count + slot * BND, BND), :] = proj
+        if sizes[slot // 2] == 2:
+            table[pl.ds(count + (slot + 1) * BND, BND), :] = proj
 
     lanes = send.shape[1]
     per = TILE * deg // lanes
@@ -232,7 +240,7 @@
                 gat[c % deg, pl.ds(dst, 1), :] = table[pl.ds(s, 1), :]
 
     def edges(t):
-        rows = pl.ds(pl.multiple_of(t * TILE, TILE), TILE)
+        rows = pl.ds(t * TILE, TILE)
         r = rcv[rows, :]
         hidden = silu(gat[0, rows, :] + r)
         for d in range(1, deg):
@@ -240,14 +248,11 @@
         agg = mm(hidden.astype(BF16), weo[...]).astype(BF16)
         pre[rows, :] = pre[rows, :] + mm(agg, wni[pl.ds(width, width), :])
 
-    def edge_step(t, carry):
-        edges(t - 1)
-        gather(t)
-        return carry
-
     with jax.named_scope("p_gather"):
         gather(0)
-        lax.fori_loop(1, count // TILE, edge_step, 0)
+        for t in range(1, count // TILE):
+            edges(t - 1)
+            gather(t)
         edges(count // TILE - 1)
 
     for j in range(zn - 1):
@@ -260,23 +265,24 @@
             @pl.when(jnp.logical_not(passed))
             def _():
                 z_recv(j).wait_recv()
-        put_kv(rc[2][pl.ds(j * ncl, ncl), :], spans[2][0] + j * ncl)
-
-    def last(t, carry):
-        rows = pl.ds(pl.multiple_of(t * TZ, TZ), TZ)
-        q = node[rows, :]
-        total = pooled[rows, :] + line(q, rows, 2)
+
+    put_kv(rc[2][...], spans[2][0])
+
+    def last_ready(rows):
+        return score(node[rows, :], *spans[2])
+
+    def last_use(rows, now):
+        total = pooled[rows, :] + line(now, rows, 2)
         att = total * lax.rsqrt(jnp.mean(total * total, axis=1, keepdims=True) + 1e-6)
         p = pre[rows, :] + mm(att.astype(BF16), wni[pl.ds(2 * width, width), :])
         update = mm(silu(p).astype(BF16), wno[...])
         cen = update - jnp.mean(update, axis=1, keepdims=True)
         var = jnp.mean(cen * cen, axis=1, keepdims=True)
         normed = cen * lax.rsqrt(var + 1e-5)
-        out_ref[rows, :] = (q.astype(F32) + normed * gain[...]).astype(BF16)
-        return carry
+        out_ref[rows, :] = (node[rows, :].astype(F32) + normed * gain[...]).astype(BF16)
 
     with jax.named_scope("p_last"):
-        lax.fori_loop(0, count // TZ, last, 0)
+        pipeline(TZ, last_ready, last_use)
 
     for group in clus_copies:
         for cp in group:
@@ -311,7 +317,7 @@
         scratch += [pltpu.VMEM(((n - 1) * ncl, width), BF16) for n in sizes]
         scratch += [
             pltpu.VMEM((6, BND, width), BF16),
-            pltpu.VMEM((total, width), BF16),
+            pltpu.VMEM((width, total), BF16),
             pltpu.VMEM((total, 2 * width), BF16),
             pltpu.VMEM((count + 6 * BND, width), F32),
             pltpu.VMEM((count, width), F32),

time: 27.3 us -> 23.5 us (0.86)
  the two profiles are of different devices: /device:TPU:1 before, /device:TPU:0 now
where the time goes in v3:
time: 23.5 us; the launch traced here: 23.4 us
  Pallas kernels  21.7 us (92%)
  local copies, waits for them, and re-layouts  1.67 us (7%)
    pallas_call x1, Pallas kernels, on_device(): pl.pallas_call(functools.partial(kernel, sizes), out_shape=jax.ShapeDtype...  21.7 us
    unnamed x1, local copies, waits for them, and re-layouts  1.67 us

profile of v3, /device:TPU:0, one launch (start us, length us, event | category | flops | bytes accessed | tf_op | source)
XLA Modules:
  0.0 23.4 jit_solution(2011324975936020881)
XLA Ops:
  0.0 21.7 %shard_map.109 = bf16[1024,128]{1,0:T(8,128)(2,1)} custom-call(bf16[1024,128]{1,0:T(8,128)(2,1)} %refs_0_.1, bf16[256,128]{1,0:T(8,128)(2,1)} %refs_1_.1, s32[32,128]{1,0:T(8,128)} %refs_2_.1, s32[8,128]{1,0:T(8,128)} %bitcast.2, bf16[128,128]{1,0:T(8,128)(2,1)} %refs_4_.1, bf16[128,128]{1,0:T(8,128)(2,1)} %refs_5_.1, bf16[256,128]{1,0:T(8,128)(2,1)} %refs_6_.1, ...), custom_call_target="tpu_custom_call" | custom-call | tf_op jit(solution)/shard_map/pallas_call | solution.py:337
  21.7 1.7 %copy.13 = bf16[1024,128]{1,0:T(8,128)(2,1)} copy(bf16[1024,128]{1,0:T(8,128)(2,1)} %shard_map.109) | data formatting | bytes 524288

commit v4 on v3

--- a/solution.py
+++ b/solution.py
@@ -50,7 +50,8 @@
     barrier = pltpu.get_barrier_semaphore()
     greeted = 0
     for axis in range(3):
-        for off in range(1, sizes[axis]):
+        near = sorted({1, sizes[2] - 1} | set(range(3, sizes[2])) | set(range(1, sizes[2] - 2)))
+        for off in range(1, sizes[axis]) if axis < 2 else near:
             pl.semaphore_signal(
                 barrier, inc=1, device_id=at(axis, off), device_id_type=pl.DeviceIdType.MESH
             )
@@ -85,11 +86,14 @@
 
     def hop(step, up):
         i = step if up else zn - 2 - step
-        j = step - 1 if up else zn - 1 - step
-        src = clus_h if step == 0 else z_slot(j)
+        far = 1 if step < 2 else step + 1
+        src = z_slot(0 if up else zn - 2) if step == 1 else clus_h
         k = 2 * step + (0 if up else 1)
-        go = jnp.logical_and(zi >= step, zi < zn - 1) if up else jnp.logical_and(zi < zn - step, zi > 0)
-        return go, remote(src, z_slot(i), zs_sem.at[k], zr_sem.at[i], at(2, 1 if up else zn - 1))
+        if step == 1:
+            go = jnp.logical_and(zi > 0, zi < zn - 1)
+        else:
+            go = zi + far < zn if up else zi >= far
+        return go, remote(src, z_slot(i), zs_sem.at[k], zr_sem.at[i], at(2, far if up else zn - far))
 
     def z_recv(i):
         return remote(clus_h, z_slot(i), zs_sem.at[0], zr_sem.at[i], at(2, 1))
@@ -100,8 +104,8 @@
 
             @pl.when(go)
             def _():
-                if step > 0:
-                    z_recv(step - 1 if up else zn - 1 - step).wait_recv()
+                if step == 1:
+                    z_recv(0 if up else zn - 2).wait_recv()
                 cp.start()
 
     def boundary(axis):
@@ -117,6 +121,8 @@
     bnd_copies = {}
     clus_copies = [[], []]
     start_hop(0)
+    for step in range(2, zn - 1):
+        start_hop(step)
     boundary(2)
     idx = 0
     for axis in (0, 1):
@@ -216,9 +222,26 @@
     with jax.named_scope("p_lines"):
         pipeline(TA, lines_ready, lines_use)
 
-    for step in range(2, zn - 1):
-        with jax.named_scope("p_hop2"):
-            start_hop(step)
+    for j in range(zn - 1):
+        with jax.named_scope("p_wz"):
+            passed = jnp.logical_and(zi > 0, zi < zn - 1) if j in (0, zn - 2) and zn > 2 else zi < 0
+
+            @pl.when(jnp.logical_not(passed))
+            def _():
+                z_recv(j).wait_recv()
+
+    put_kv(rc[2][...], spans[2][0])
+
+    def last_ready(rows):
+        return score(node[rows, :], *spans[2])
+
+    def last_use(rows, now):
+        total = pooled[rows, :] + line(now, rows, 2)
+        att = total * lax.rsqrt(jnp.mean(total * total, axis=1, keepdims=True) + 1e-6)
+        pre[rows, :] = pre[rows, :] + mm(att.astype(BF16), wni[pl.ds(2 * width, width), :])
+
+    with jax.named_scope("p_zline"):
+        pipeline(TZ, last_ready, last_use)
 
     with jax.named_scope("p_wb"):
         for cp in bnd_copies.values():
@@ -248,41 +271,23 @@
         agg = mm(hidden.astype(BF16), weo[...]).astype(BF16)
         pre[rows, :] = pre[rows, :] + mm(agg, wni[pl.ds(width, width), :])
 
-    with jax.named_scope("p_gather"):
-        gather(0)
-        for t in range(1, count // TILE):
-            edges(t - 1)
-            gather(t)
-        edges(count // TILE - 1)
-
-    for j in range(zn - 1):
-        with jax.named_scope("p_wz"):
-            passed = jnp.logical_or(
-                jnp.logical_and(j < zi, jnp.logical_and(zi < zn - 1, j < zn - 2)),
-                jnp.logical_and(j >= zi, jnp.logical_and(zi > 0, j > 0)),
-            )
-
-            @pl.when(jnp.logical_not(passed))
-            def _():
-                z_recv(j).wait_recv()
-
-    put_kv(rc[2][...], spans[2][0])
-
-    def last_ready(rows):
-        return score(node[rows, :], *spans[2])
-
-    def last_use(rows, now):
-        total = pooled[rows, :] + line(now, rows, 2)
-        att = total * lax.rsqrt(jnp.mean(total * total, axis=1, keepdims=True) + 1e-6)
-        p = pre[rows, :] + mm(att.astype(BF16), wni[pl.ds(2 * width, width), :])
-        update = mm(silu(p).astype(BF16), wno[...])
+    def nodes(t):
+        rows = pl.ds(t * TILE, TILE)
+        update = mm(silu(pre[rows, :]).astype(BF16), wno[...])
         cen = update - jnp.mean(update, axis=1, keepdims=True)
         var = jnp.mean(cen * cen, axis=1, keepdims=True)
         normed = cen * lax.rsqrt(var + 1e-5)
         out_ref[rows, :] = (node[rows, :].astype(F32) + normed * gain[...]).astype(BF16)
 
-    with jax.named_scope("p_last"):
-        pipeline(TZ, last_ready, last_use)
+    with jax.named_scope("p_gather"):
+        tiles = count // TILE
+        for t in range(tiles + 2):
+            if t >= 2:
+                nodes(t - 2)
+            if 1 <= t <= tiles:
+                edges(t - 1)
+            if t < tiles:
+                gather(t)
 
     for group in clus_copies:
         for cp in group:

time: 23.5 us -> 23.6 us (level)
  no operation moved by 1% of the time
where the time goes in v4:
time: 23.6 us; the launch traced here: 23.5 us
  Pallas kernels  21.8 us (92%)
  local copies, waits for them, and re-layouts  1.67 us (7%)
    pallas_call x1, Pallas kernels, on_device(): pl.pallas_call(functools.partial(kernel, sizes), out_shape=jax.ShapeDtype...  21.8 us
    unnamed x1, local copies, waits for them, and re-layouts  1.67 us

profile of v4, /device:TPU:0, one launch (start us, length us, event | category | flops | bytes accessed | tf_op | source)
XLA Modules:
  0.0 23.5 jit_solution(12354770486735576964)
XLA Ops:
  0.0 21.8 %shard_map.109 = bf16[1024,128]{1,0:T(8,128)(2,1)} custom-call(bf16[1024,128]{1,0:T(8,128)(2,1)} %refs_0_.1, bf16[256,128]{1,0:T(8,128)(2,1)} %refs_1_.1, s32[32,128]{1,0:T(8,128)} %refs_2_.1, s32[8,128]{1,0:T(8,128)} %bitcast.2, bf16[128,128]{1,0:T(8,128)(2,1)} %refs_4_.1, bf16[128,128]{1,0:T(8,128)(2,1)} %refs_5_.1, bf16[256,128]{1,0:T(8,128)(2,1)} %refs_6_.1, ...), custom_call_target="tpu_custom_call" | custom-call | tf_op jit(solution)/shard_map/pallas_call | solution.py:342
  21.8 1.7 %copy.13 = bf16[1024,128]{1,0:T(8,128)(2,1)} copy(bf16[1024,128]{1,0:T(8,128)(2,1)} %shard_map.109) | data formatting | bytes 524288
